TPU v7x, 32 devices: a whole 2x2x4 slice. The times are simulated.
32 devices in a mesh: cls: 32 (over z, y, x, core).
Axes of the slice: x: 2, y: 2, z: 4, core: 2. Of those that a mesh axis runs over, the one named last changes fastest.
Arguments:
- features: bfloat16 [512, 12544], P('cls'), may hold values from -6 to 6
- fc_weight: bfloat16 [12544, 512], replicated, may hold values from -0.0546875 to 0.0546875
- centers: bfloat16 [131072, 512], P('cls'), may hold values from -6 to 6
- labels: int32 [512], replicated, may hold values from 0 to 131071
Outputs:
- loss: float32 [512], P('cls')
- grad_centers: bfloat16 [131072, 512], P('cls')
- grad_fc: float32 [12544, 512], P('cls')
All inputs are finite; a program needn't handle non-finite values.
Results may differ from a plain program's by a relative error of at most 0.0078.
Values may be sent and summed in bfloat16 or wider, within the bound.
A program may use at most 128 MiB of HBM per device.

v0:
```python
import math
import jax
import jax.numpy as jnp
from jax import lax
from jax.sharding import PartitionSpec as P

logit_scale = 64.0
cos_margin = math.cos(0.5)
sin_margin = math.sin(0.5)
epsilon = 1e-06


def inverse_norm(values):
    return lax.rsqrt(jnp.sum(values * values, axis=1, keepdims=True) + epsilon)


def margin_logits(emb_low, center_low, labels, offset):
    cosines = lax.dot_general(
        emb_low, center_low, (((1,), (1,)), ((), ())), preferred_element_type=jnp.float32
    )
    local_ids = labels - offset
    is_target = local_ids[:, None] == lax.broadcasted_iota(jnp.int32, (1, center_low.shape[0]), 1)
    target_cos = jnp.sum(jnp.where(is_target, cosines, 0.0), axis=1)
    target_sine = jnp.sqrt(1.0 - target_cos * target_cos)
    margined = target_cos * cos_margin - target_sine * sin_margin
    logits = logit_scale * jnp.where(is_target, margined[:, None], cosines)
    slope = cos_margin + sin_margin * target_cos / target_sine
    return (logits, is_target, slope)


def swap(blocks):
    return lax.all_to_all(blocks, "cls", split_axis=0, concat_axis=0, tiled=True)


def spread(block, count):
    return swap(jnp.broadcast_to(block[None], (count, *block.shape)))


def on_device(features, fc_weight, centers, labels):
    tok_rows = features.shape[0]
    class_rows = centers.shape[0]
    my_index = lax.axis_index("cls")
    count = lax.axis_size("cls")
    columns = lax.all_to_all(features, "cls", split_axis=1, concat_axis=0, tiled=True)
    embedded = jnp.dot(features, fc_weight, preferred_element_type=jnp.float32).astype(jnp.bfloat16)
    gathered = spread(embedded, count).reshape(count * tok_rows, -1)
    all_float = gathered.astype(jnp.float32)
    emb_low = (all_float * inverse_norm(all_float)).astype(jnp.bfloat16)
    own_float = embedded.astype(jnp.float32)
    inv_emb = inverse_norm(own_float)
    emb_dir = own_float * inv_emb
    center_float = centers.astype(jnp.float32)
    inv_center = inverse_norm(center_float)
    center_dir = center_float * inv_center
    center_low = center_dir.astype(jnp.bfloat16)
    logits, is_target, slope = margin_logits(emb_low, center_low, labels, my_index * class_rows)
    target_logit = jnp.sum(jnp.where(is_target, logits, 0.0), axis=1)
    stats = jnp.stack([jnp.sum(jnp.exp(logits - logit_scale), axis=1), target_logit])
    row_total, target_all = jnp.sum(spread(stats, count), axis=0)
    log_total = logit_scale + jnp.log(row_total)
    loss = lax.dynamic_slice_in_dim(log_total - target_all, my_index * tok_rows, tok_rows)
    probs = jnp.exp(logits - log_total[:, None])
    grad_cos = (
        logit_scale
        * (probs - is_target.astype(jnp.float32))
        * jnp.where(is_target, slope[:, None], 1.0)
    ).astype(jnp.bfloat16)
    grad_unit = lax.dot_general(
        grad_cos, emb_low, (((0,), (0,)), ((), ())), preferred_element_type=jnp.float32
    )
    grad_centers = (
        (grad_unit - center_dir * jnp.sum(grad_unit * center_dir, axis=1, keepdims=True))
        * inv_center
    ).astype(jnp.bfloat16)
    partial = jnp.dot(grad_cos, center_low, preferred_element_type=jnp.float32)
    parts = swap(partial.astype(jnp.bfloat16).reshape(count, tok_rows, -1))
    grad_dir = jnp.sum(parts.astype(jnp.float32), axis=0)
    grad_emb = (
        (grad_dir - emb_dir * jnp.sum(grad_dir * emb_dir, axis=1, keepdims=True)) * inv_emb
    ).astype(jnp.bfloat16)
    all_grads = spread(grad_emb, count).reshape(count * tok_rows, -1)
    grad_fc = lax.dot_general(
        columns, all_grads, (((0,), (0,)), ((), ())), preferred_element_type=jnp.float32
    )
    return (loss, grad_centers, grad_fc)


def solution(mesh):
    placed = (P("cls", None), P(), P("cls", None), P())
    return jax.shard_map(
        on_device,
        mesh=mesh,
        in_specs=placed,
        out_specs=(P("cls"), P("cls", None), P("cls", None)),
        check_vma=False,
    )
```

profile of v0, /device:TPU:0, one launch (start us, length us, event | category | flops | bytes accessed | tf_op | source)
XLA Modules:
  0.0 122.4 jit_solution(10489114198073126917)
XLA Ops:
  0.6 6.7 %fusion.23 = (f32[16]{0:T(128)S(1)}, bf16[16,512]{1,0:T(8,128)(2,1)S(1)}) fusion(bf16[16,12544]{1,0:T(8,128)(2,1)} %param.4, bf16[12544,512]{1,0:T(8,128)(2,1)} %param.5), kind=kOutput, calls=%fused_computation.34 | convolution fusion | flops 205553648 | bytes 13262912 | tf_op jit(solution)/shard_map/dot_general | solution.py:45
  7.3 0.9 broadcast_in_dim.31
  8.2 7.3 %all-to-all-start = ((bf16[32,16,512]{2,1,0:T(8,128)(2,1)}), bf16[32,16,512]{2,1,0:T(8,128)(2,1)S(1)}, u32[]{:S(2)}, u32[]{:S(2)}) async-start(bf16[32,16,512]{2,1,0:T(8,128)(2,1)} %broadcast_in_dim.31), calls=%async_computation | async-start | bytes 1048576 | tf_op jit(solution)/shard_map/all_to_all | solution.py:32
  15.5 6.3 %copy.21 = bf16[4096,512]{0,1:T(8,128)(2,1)} copy(bf16[4096,512]{1,0:T(8,128)(2,1)} %param.6) | data formatting | bytes 8388608 | tf_op args[2]
  21.8 3.1 %fusion.7 = f32[4096]{0:T(1024)S(1)} fusion(bf16[4096,512]{0,1:T(8,128)(2,1)} %copy.21), kind=kLoop, calls=%fused_computation.9 | loop fusion | flops 6287360 | bytes 4210688 | tf_op jit(solution)/shard_map/reduce_sum | solution.py:14
  24.9 6.2 %all-to-all-done = bf16[32,16,512]{2,1,0:T(8,128)(2,1)S(1)} async-done(((bf16[32,16,512]{2,1,0:T(8,128)(2,1)}), bf16[32,16,512]{2,1,0:T(8,128)(2,1)S(1)}, u32[]{:S(2)}, u32[]{:S(2)}) %all-to-all-start) | async-done | bytes 524320 | tf_op jit(solution)/shard_map/all_to_all | solution.py:32
  31.1 0.2 multiply_reduce_fusion
  31.3 0.1 rsqrt.32
  31.4 0.2 fusion.15
  31.6 4.9 %select_reduce_fusion.1 = (f32[512]{0:T(512)S(1)}, f32[512,4096]{1,0:T(8,128)S(1)}) fusion(s32[512]{0:T(512)S(1)} %broadcast_subtract_fusion, bf16[512,512]{1,0:T(8,128)(2,1)S(1)} %fusion.15, bf16[4096,512]{0,1:T(8,128)(2,1)} %copy.21, f32[4096]{0:T(1024)S(1)} %add_rsqrt_fusion), kind=kOutput, calls=%fused_computation.14 | convolution fusion | flops 2160066048 | bytes 13127680 | tf_op jit(solution)/shard_map/dot_general | solution.py:18
  36.5 3.2 %copy-done.1 = f32[512,4096]{1,0:T(8,128)} copy-done((f32[512,4096]{1,0:T(8,128)}, f32[512,4096]{1,0:T(8,128)S(1)}, u32[]{:S(2)}) %copy-start.1) | copy-done | bytes 8388632
  39.7 4.0 %exponential_reduce_fusion = (f32[512]{0:T(512)S(1)}, f32[512]{0:T(512)S(1)}) fusion(f32[512,4096]{1,0:T(8,128)S(1)} %get-tuple-element.28, f32[512]{0:T(512)S(1)} %get-tuple-element.26, s32[512]{0:T(512)S(1)} %broadcast_subtract_fusion), kind=kLoop, calls=%fused_computation.12 | loop fusion | flops 14679040 | bytes 8396800 | tf_op jit(solution)/shard_map/reduce_sum | solution.py:58
  43.8 11.0 %all_to_all.36 = f32[32,2,512]{2,1,0:T(2,128)S(1)} all-to-all(f32[32,2,512]{2,1,0:T(2,128)S(1)} %broadcast_in_dim.34), channel_id=1, replica_groups=mesh['cls'=32] {'cls'}, dimensions={0} | all-to-all | bytes 262144 | tf_op jit(solution)/shard_map/all_to_all | solution.py:32
  54.9 6.8 %multiply_convert_fusion = bf16[512,4096]{1,0:T(8,128)(2,1)S(1)} fusion(f32[512,4096]{1,0:T(8,128)} %copy-done.1, f32[512]{0:T(512)S(1)} %get-tuple-element.25, f32[512]{0:T(512)S(1)} %bitcast.23, f32[512]{0:T(512)S(1)} %get-tuple-element.26, s32[512]{0:T(512)S(1)} %broadcast_subtract_fusion), kind=kLoop, calls=%fused_computation.10 | loop fusion | flops 20971520 | bytes 12591104 | tf_op jit(solution)/shard_map/convert_element_type | solution.py:67
  61.7 3.2 %fusion.12 = bf16[512,512]{1,0:T(8,128)(2,1)} fusion(bf16[512,4096]{1,0:T(8,128)(2,1)S(1)} %multiply_convert_fusion, bf16[4096,512]{0,1:T(8,128)(2,1)S(1)} %copy-done, f32[4096]{0:T(1024)S(1)} %add_rsqrt_fusion), kind=kOutput, calls=%fused_computation.19 | convolution fusion | flops 2154037248 | bytes 8929280 | tf_op jit(solution)/shard_map/dot_general | solution.py:75
  64.9 2.6 %all-to-all-start.2 = ((bf16[32,16,512]{2,1,0:T(8,128)(2,1)}), bf16[32,16,512]{2,1,0:T(8,128)(2,1)S(1)}, u32[]{:S(2)}, u32[]{:S(2)}) async-start(bf16[32,16,512]{2,1,0:T(8,128)(2,1)} %bitcast.5), calls=%async_computation.2 | async-start | bytes 1048576 | tf_op jit(solution)/shard_map/all_to_all | solution.py:32
  67.5 1.2 all_to_all.28
  68.7 1.1 copy.23
  69.9 13.3 %all-to-all-done.2 = bf16[32,16,512]{2,1,0:T(8,128)(2,1)S(1)} async-done(((bf16[32,16,512]{2,1,0:T(8,128)(2,1)}), bf16[32,16,512]{2,1,0:T(8,128)(2,1)S(1)}, u32[]{:S(2)}, u32[]{:S(2)}) %all-to-all-start.2) | async-done | bytes 524320 | tf_op jit(solution)/shard_map/all_to_all | solution.py:32
  83.1 2.9 %all-to-all-start.4 = ((bf16[16,32,392]{2,0,1:T(8,128)(2,1)}), bf16[16,32,392]{2,0,1:T(8,128)(2,1)S(1)}, u32[]{:S(2)}, u32[]{:S(2)}) async-start(bf16[16,32,392]{2,0,1:T(8,128)(2,1)} %copy.23), calls=%async_computation.4 | async-start | bytes 1048576 | tf_op jit(solution)/shard_map/all_to_all | solution.py:44
  86.0 9.5 %fusion.3 = (f32[4096]{0:T(1024)S(1)}, f32[4096,512]{0,1:T(8,128)}) fusion(bf16[4096,512]{0,1:T(8,128)(2,1)} %copy.21, f32[4096]{0:T(1024)S(1)} %add_rsqrt_fusion, bf16[512,4096]{1,0:T(8,128)(2,1)} %copy-done.2, bf16[512,512]{1,0:T(8,128)(2,1)S(1)} %fusion.15), kind=kOutput, calls=%fused_computation.5 | convolution fusion | flops 2155868160 | bytes 17334272 | tf_op jit(solution)/shard_map/dot_general | solution.py:68
  95.5 0.1 convert_reduce_fusion
  95.6 0.2 fusion.19
  95.8 0.1 fusion.22
  95.8 5.8 %all-to-all-done.4 = bf16[16,32,392]{2,0,1:T(8,128)(2,1)S(1)} async-done(((bf16[16,32,392]{2,0,1:T(8,128)(2,1)}), bf16[16,32,392]{2,0,1:T(8,128)(2,1)S(1)}, u32[]{:S(2)}, u32[]{:S(2)}) %all-to-all-start.4) | async-done | bytes 401440 | tf_op jit(solution)/shard_map/all_to_all | solution.py:44
  101.6 0.9 broadcast_in_dim.58
  102.5 3.0 %all-to-all-start.3 = ((bf16[32,16,512]{2,1,0:T(8,128)(2,1)}), bf16[32,16,512]{2,1,0:T(8,128)(2,1)S(1)}, u32[]{:S(2)}, u32[]{:S(2)}) async-start(bf16[32,16,512]{2,1,0:T(8,128)(2,1)} %broadcast_in_dim.58), calls=%async_computation.3 | async-start | bytes 1048576 | tf_op jit(solution)/shard_map/all_to_all | solution.py:32
  105.5 8.3 %fusion.6 = bf16[4096,512]{0,1:T(8,128)(2,1)} fusion(f32[4096,512]{0,1:T(8,128)} %get-tuple-element.30, bf16[4096,512]{0,1:T(8,128)(2,1)} %copy.21, f32[4096]{0:T(1024)S(1)} %get-tuple-element.29, f32[4096]{0:T(1024)S(1)} %add_rsqrt_fusion), kind=kLoop, calls=%fused_computation.8 | loop fusion | flops 12582912 | bytes 16809984 | tf_op jit(solution)/shard_map/convert_element_type | solution.py:74
  113.8 6.4 %copy.24 = bf16[4096,512]{1,0:T(8,128)(2,1)} copy(bf16[4096,512]{0,1:T(8,128)(2,1)} %fusion.6) | data formatting | bytes 8388608
  120.2 0.6 dynamic_slice.3
  120.7 0.3 all-to-all-done.3
  121.1 1.3 %convolution_bitcast_fusion = f32[392,512]{1,0:T(8,128)} fusion(bf16[32,16,512]{2,1,0:T(8,128)(2,1)S(1)} %all-to-all-done.3, bf16[16,32,392]{2,0,1:T(8,128)(2,1)S(1)} %all-to-all-done.4), kind=kOutput, calls=%fused_computation.18 | convolution fusion | flops 205520896 | bytes 1728512 | tf_op jit(solution)/shard_map/dot_general | solution.py:82
  (19 shorter events, 0.2 us)
Async XLA Ops:
  7.3 14.5 %copy-start.4 = (s32[512]{0:T(512)S(1)}, s32[512]{0:T(512)}, u32[]{:S(2)}) copy-start(s32[512]{0:T(512)} %param.7) | copy-start | bytes 6148
  8.2 22.9 %all-to-all-start = ((bf16[32,16,512]{2,1,0:T(8,128)(2,1)}), bf16[32,16,512]{2,1,0:T(8,128)(2,1)S(1)}, u32[]{:S(2)}, u32[]{:S(2)}) async-start(bf16[32,16,512]{2,1,0:T(8,128)(2,1)} %broadcast_in_dim.31), calls=%async_computation | async-start | bytes 1048576 | tf_op jit(solution)/shard_map/all_to_all | solution.py:32
  36.5 3.2 %copy-start.1 = (f32[512,4096]{1,0:T(8,128)}, f32[512,4096]{1,0:T(8,128)S(1)}, u32[]{:S(2)}) copy-start(f32[512,4096]{1,0:T(8,128)S(1)} %get-tuple-element.28) | copy-start | bytes 25165828
  54.9 6.8 %copy-start = (bf16[4096,512]{0,1:T(8,128)(2,1)S(1)}, bf16[4096,512]{0,1:T(8,128)(2,1)}, u32[]{:S(2)}) copy-start(bf16[4096,512]{0,1:T(8,128)(2,1)} %copy.21) | copy-start | bytes 12582916
  61.7 3.2 %copy-start.2 = (bf16[512,4096]{1,0:T(8,128)(2,1)}, bf16[512,4096]{1,0:T(8,128)(2,1)S(1)}, u32[]{:S(2)}) copy-start(bf16[512,4096]{1,0:T(8,128)(2,1)S(1)} %multiply_convert_fusion) | copy-start | bytes 12582916
  61.7 5.8 %copy-start.3 = (bf16[16,12544]{1,0:T(8,128)(2,1)S(1)}, bf16[16,12544]{1,0:T(8,128)(2,1)}, u32[]{:S(2)}) copy-start(bf16[16,12544]{1,0:T(8,128)(2,1)} %param.4) | copy-start | bytes 1204228
  64.9 18.2 %all-to-all-start.2 = ((bf16[32,16,512]{2,1,0:T(8,128)(2,1)}), bf16[32,16,512]{2,1,0:T(8,128)(2,1)S(1)}, u32[]{:S(2)}, u32[]{:S(2)}) async-start(bf16[32,16,512]{2,1,0:T(8,128)(2,1)} %bitcast.5), calls=%async_computation.2 | async-start | bytes 1048576 | tf_op jit(solution)/shard_map/all_to_all | solution.py:32
  83.1 18.5 %all-to-all-start.4 = ((bf16[16,32,392]{2,0,1:T(8,128)(2,1)}), bf16[16,32,392]{2,0,1:T(8,128)(2,1)S(1)}, u32[]{:S(2)}, u32[]{:S(2)}) async-start(bf16[16,32,392]{2,0,1:T(8,128)(2,1)} %copy.23), calls=%async_computation.4 | async-start | bytes 1048576 | tf_op jit(solution)/shard_map/all_to_all | solution.py:44
  102.5 18.6 %all-to-all-start.3 = ((bf16[32,16,512]{2,1,0:T(8,128)(2,1)}), bf16[32,16,512]{2,1,0:T(8,128)(2,1)S(1)}, u32[]{:S(2)}, u32[]{:S(2)}) async-start(bf16[32,16,512]{2,1,0:T(8,128)(2,1)} %broadcast_in_dim.58), calls=%async_computation.3 | async-start | bytes 1048576 | tf_op jit(solution)/shard_map/all_to_all | solution.py:32
where the time goes:
time: 123 us; the launch traced here: 122 us
  waiting for transfers between devices  25.6 us (21%)
  matrix products  25.5 us (21%)
  other arithmetic  23 us (19%)
  local copies, waits for them, and re-layouts  20.7 us (17%)
  starting transfers between devices  15.8 us (13%)
  blocking collectives  11 us (9%)
    all_to_all x3, waiting for transfers between devices, swap(): lax.all_to_all(blocks, 'cls', split_axis=0, concat_axis=0, tiled=True)  19.8 us
    unnamed x12, local copies, waits for them, and re-layouts  16 us
    all_to_all x3, starting transfers between devices, swap(): lax.all_to_all(blocks, 'cls', split_axis=0, concat_axis=0, tiled=True)  12.9 us
    all_to_all x1, blocking collectives, swap(): lax.all_to_all(blocks, 'cls', split_axis=0, concat_axis=0, tiled=True)  11 us
    dot_general x1, matrix products, on_device(): lax.dot_general(grad_cos, emb_low, (((0,), (0,)), ((), ())), preferred_el...  9.45 us
    convert_element_type x1, other arithmetic, on_device(): grad_centers = ((grad_unit - center_dir * jnp.sum(grad_unit * center_dir,...  8.29 us
    convert_element_type x1, other arithmetic, on_device(): grad_cos = (logit_scale * (probs - is_target.astype(jnp.float32)) * jnp.w...  6.78 us
    dot_general x1, matrix products, on_device(): jnp.dot(features, fc_weight, preferred_element_type=jnp.float32)  6.67 us
  transfers between devices with their start and end apart: 4, of which 4 were waited for; matrix products, arithmetic and copies ran while one was open for 29% of the time, Pallas kernels for 0%

commit v1 on v0

--- a/solution.py
+++ b/solution.py
@@ -8,6 +8,15 @@
 cos_margin = math.cos(0.5)
 sin_margin = math.sin(0.5)
 epsilon = 1e-06
+
+
+def show_records(vals, net_axis):
+    even = lax.axis_size(net_axis)
+    d_next = jnp.split(vals, even, axis=1)
+    answer = jnp.stack(d_next, axis=0)
+    outcome_arr = lax.all_to_all(answer, net_axis, 0, 0)
+    base_arr = jnp.concatenate(outcome_arr, axis=0)
+    return base_arr
 
 
 def inverse_norm(values):
@@ -41,7 +50,7 @@
     class_rows = centers.shape[0]
     my_index = lax.axis_index("cls")
     count = lax.axis_size("cls")
-    columns = lax.all_to_all(features, "cls", split_axis=1, concat_axis=0, tiled=True)
+    columns = show_records(features, net_axis="cls")
     embedded = jnp.dot(features, fc_weight, preferred_element_type=jnp.float32).astype(jnp.bfloat16)
     gathered = spread(embedded, count).reshape(count * tok_rows, -1)
     all_float = gathered.astype(jnp.float32)

time: 123 us -> 138 us (1.12)
  local copies, waits for them, and re-layouts: 20.7 us -> 40.5 us
  blocking collectives: 11 us -> 0 us
  starting transfers between devices: 15.8 us -> 21.8 us
    unnamed x12 -> x43, local copies, waits for them, and re-layouts: 16 us -> 36.7 us
    all_to_all x1 -> x0, blocking collectives: 11 us -> none  [swap(): lax.all_to_all(blocks, 'cls', split_axis=0, concat_axis=0, tiled=True)]
    all_to_all x3 -> x4, starting transfers between devices: 12.9 us -> 18.9 us  [swap(): lax.all_to_all(blocks, 'cls', split_axis=0, concat_axis=0, tiled=True)]
    all_to_all x2 -> x0, local copies, waits for them, and re-layouts: 2.32 us -> none  [on_device(): lax.all_to_all(features, 'cls', split_axis=1, concat_axis=0, tiled=True)]
    all_to_all x3 -> x4, waiting for transfers between devices: 19.8 us -> 19.9 us  [swap(): lax.all_to_all(blocks, 'cls', split_axis=0, concat_axis=0, tiled=True)]
  transfers between devices with their start and end apart: 4 -> 5, of which waited for: 4 -> 4; matrix products, arithmetic and copies ran while one was open for 29% -> 41% of each run, Pallas kernels for 0% -> 0%
where the time goes in v1:
time: 138 us; the launch traced here: 137 us
  local copies, waits for them, and re-layouts  40.5 us (29%)
  waiting for transfers between devices  25.7 us (19%)
  matrix products  25.6 us (19%)
  other arithmetic  23 us (17%)
  starting transfers between devices  21.8 us (16%)
    unnamed x43, local copies, waits for them, and re-layouts  36.7 us
    all_to_all x4, waiting for transfers between devices, swap(): lax.all_to_all(blocks, 'cls', split_axis=0, concat_axis=0, tiled=True)  19.9 us
    all_to_all x4, starting transfers between devices, swap(): lax.all_to_all(blocks, 'cls', split_axis=0, concat_axis=0, tiled=True)  18.9 us
    dot_general x1, matrix products, on_device(): lax.dot_general(grad_cos, emb_low, (((0,), (0,)), ((), ())), preferred_el...  9.48 us
    convert_element_type x1, other arithmetic, on_device(): grad_centers = ((grad_unit - center_dir * jnp.sum(grad_unit * center_dir,...  8.29 us
    convert_element_type x1, other arithmetic, on_device(): grad_cos = (logit_scale * (probs - is_target.astype(jnp.float32)) * jnp.w...  6.78 us
    dot_general x1, matrix products, on_device(): jnp.dot(features, fc_weight, preferred_element_type=jnp.float32)  6.7 us
    all_to_all x1, waiting for transfers between devices, show_records(): outcome_arr = lax.all_to_all(answer, net_axis, 0, 0)  5.78 us
  transfers between devices with their start and end apart: 5, of which 4 were waited for; matrix products, arithmetic and copies ran while one was open for 41% of the time, Pallas kernels for 0%

profile of v1, /device:TPU:0, one launch (start us, length us, event | category | flops | bytes accessed | tf_op | source)
XLA Modules:
  0.0 137.4 jit_solution(16446296759329911950)
XLA Ops:
  0.6 6.7 %fusion.22 = (f32[16]{0:T(128)S(1)}, bf16[16,512]{1,0:T(8,128)(2,1)S(1)}) fusion(bf16[16,12544]{1,0:T(8,128)(2,1)} %param.4, bf16[12544,512]{1,0:T(8,128)(2,1)} %param.5), kind=kOutput, calls=%fused_computation.65 | convolution fusion | flops 205553648 | bytes 13262912 | tf_op jit(solution)/shard_map/dot_general | solution.py:54
  7.4 0.9 broadcast_in_dim.31
  8.2 7.3 %all-to-all-start = ((bf16[32,16,512]{2,1,0:T(8,128)(2,1)}), bf16[32,16,512]{2,1,0:T(8,128)(2,1)S(1)}, u32[]{:S(2)}, u32[]{:S(2)}) async-start(bf16[32,16,512]{2,1,0:T(8,128)(2,1)} %broadcast_in_dim.31), calls=%async_computation | async-start | bytes 1048576 | tf_op jit(solution)/shard_map/all_to_all | solution.py:41
  16.8 0.7 constant_dynamic-update-slice_fusion.29
  19.5 0.7 constant_dynamic-update-slice_fusion.25
  22.2 0.7 constant_dynamic-update-slice_fusion.21
  25.6 0.7 constant_dynamic-update-slice_fusion.16
  28.3 0.7 constant_dynamic-update-slice_fusion.12
  31.0 0.7 constant_dynamic-update-slice_fusion.8
  32.3 6.3 %copy.49 = bf16[4096,512]{0,1:T(8,128)(2,1)} copy(bf16[4096,512]{1,0:T(8,128)(2,1)} %param.6) | data formatting | bytes 8388608 | tf_op args[2]
  39.3 3.1 %fusion.7 = f32[4096]{0:T(1024)S(1)} fusion(bf16[4096,512]{0,1:T(8,128)(2,1)} %copy.49), kind=kLoop, calls=%fused_computation.9 | loop fusion | flops 6287360 | bytes 4210688 | tf_op jit(solution)/shard_map/reduce_sum | solution.py:23
  42.9 4.9 %select_reduce_fusion.1 = (f32[512]{0:T(512)S(1)}, f32[512,4096]{1,0:T(8,128)S(1)}) fusion(s32[512]{0:T(512)S(1)} %broadcast_subtract_fusion, bf16[512,512]{1,0:T(8,128)(2,1)S(1)} %fusion.15, bf16[4096,512]{0,1:T(8,128)(2,1)} %copy.49, f32[4096]{0:T(1024)S(1)} %add_rsqrt_fusion), kind=kOutput, calls=%fused_computation.14 | convolution fusion | flops 2160066048 | bytes 13127680 | tf_op jit(solution)/shard_map/dot_general | solution.py:27
  47.8 3.2 %copy-done.1 = f32[512,4096]{1,0:T(8,128)} copy-done((f32[512,4096]{1,0:T(8,128)}, f32[512,4096]{1,0:T(8,128)S(1)}, u32[]{:S(2)}) %copy-start.1) | copy-done | bytes 8388632
  51.0 4.0 %exponential_reduce_fusion = (f32[512]{0:T(512)S(1)}, f32[512]{0:T(512)S(1)}) fusion(f32[512,4096]{1,0:T(8,128)S(1)} %get-tuple-element.25, f32[512]{0:T(512)S(1)} %get-tuple-element.23, s32[512]{0:T(512)S(1)} %broadcast_subtract_fusion), kind=kLoop, calls=%fused_computation.12 | loop fusion | flops 14679040 | bytes 8396800 | tf_op jit(solution)/shard_map/reduce_sum | solution.py:67
  55.1 0.7 broadcast_in_dim.34
  55.8 6.0 %all-to-all-start.1 = ((f32[32,2,512]{2,1,0:T(2,128)}), f32[32,2,512]{2,1,0:T(2,128)S(1)}, u32[]{:S(2)}, u32[]{:S(2)}) async-start(f32[32,2,512]{2,1,0:T(2,128)} %broadcast_in_dim.34), calls=%async_computation.1 | async-start | bytes 262144 | tf_op jit(solution)/shard_map/all_to_all | solution.py:41
  62.5 0.7 constant_dynamic-update-slice_fusion.4
  63.1 6.7 %all-to-all-done.1 = f32[32,2,512]{2,1,0:T(2,128)S(1)} async-done(((f32[32,2,512]{2,1,0:T(2,128)}), f32[32,2,512]{2,1,0:T(2,128)S(1)}, u32[]{:S(2)}, u32[]{:S(2)}) %all-to-all-start.1) | async-done | bytes 131104 | tf_op jit(solution)/shard_map/all_to_all | solution.py:41
  69.9 6.8 %multiply_convert_fusion = bf16[512,4096]{1,0:T(8,128)(2,1)S(1)} fusion(f32[512,4096]{1,0:T(8,128)} %copy-done.1, f32[512]{0:T(512)S(1)} %get-tuple-element.22, f32[512]{0:T(512)S(1)} %bitcast.83, f32[512]{0:T(512)S(1)} %get-tuple-element.23, s32[512]{0:T(512)S(1)} %broadcast_subtract_fusion), kind=kLoop, calls=%fused_computation.10 | loop fusion | flops 20971520 | bytes 12591104 | tf_op jit(solution)/shard_map/convert_element_type | solution.py:76
  76.7 3.2 %fusion.12 = bf16[512,512]{1,0:T(8,128)(2,1)} fusion(bf16[512,4096]{1,0:T(8,128)(2,1)S(1)} %multiply_convert_fusion, bf16[4096,512]{0,1:T(8,128)(2,1)S(1)} %copy-done, f32[4096]{0:T(1024)S(1)} %add_rsqrt_fusion), kind=kOutput, calls=%fused_computation.19 | convolution fusion | flops 2154037248 | bytes 8929280 | tf_op jit(solution)/shard_map/dot_general | solution.py:84
  79.9 2.6 %all-to-all-start.3 = ((bf16[32,16,512]{2,1,0:T(8,128)(2,1)}), bf16[32,16,512]{2,1,0:T(8,128)(2,1)S(1)}, u32[]{:S(2)}, u32[]{:S(2)}) async-start(bf16[32,16,512]{2,1,0:T(8,128)(2,1)} %bitcast.37), calls=%async_computation.3 | async-start | bytes 1048576 | tf_op jit(solution)/shard_map/all_to_all | solution.py:41
  83.2 0.7 constant_dynamic-update-slice_fusion.2
  84.5 0.7 constant_dynamic-update-slice_fusion
  85.2 12.9 %all-to-all-done.3 = bf16[32,16,512]{2,1,0:T(8,128)(2,1)S(1)} async-done(((bf16[32,16,512]{2,1,0:T(8,128)(2,1)}), bf16[32,16,512]{2,1,0:T(8,128)(2,1)S(1)}, u32[]{:S(2)}, u32[]{:S(2)}) %all-to-all-start.3) | async-done | bytes 524320 | tf_op jit(solution)/shard_map/all_to_all | solution.py:41
  98.1 2.9 %all-to-all-start.2 = ((bf16[32,16,392]{2,1,0:T(8,128)(2,1)}), bf16[32,16,392]{2,1,0:T(8,128)(2,1)S(1)}, u32[]{:S(2)}, u32[]{:S(2)}) async-start(bf16[32,16,392]{2,1,0:T(8,128)(2,1)} %constant_dynamic-update-slice_fusion), calls=%async_computation.2 | async-start | bytes 1048576 | tf_op jit(solution)/shard_map/all_to_all | solution.py:17
  101.0 9.5 %fusion.3 = (f32[4096]{0:T(1024)S(1)}, f32[4096,512]{0,1:T(8,128)}) fusion(bf16[4096,512]{0,1:T(8,128)(2,1)} %copy.49, f32[4096]{0:T(1024)S(1)} %add_rsqrt_fusion, bf16[512,4096]{1,0:T(8,128)(2,1)} %copy-done.2, bf16[512,512]{1,0:T(8,128)(2,1)S(1)} %fusion.15), kind=kOutput, calls=%fused_computation.5 | convolution fusion | flops 2155868160 | bytes 17334272 | tf_op jit(solution)/shard_map/dot_general | solution.py:77
  110.8 5.8 %all-to-all-done.2 = bf16[32,16,392]{2,1,0:T(8,128)(2,1)S(1)} async-done(((bf16[32,16,392]{2,1,0:T(8,128)(2,1)}), bf16[32,16,392]{2,1,0:T(8,128)(2,1)S(1)}, u32[]{:S(2)}, u32[]{:S(2)}) %all-to-all-start.2) | async-done | bytes 401440 | tf_op jit(solution)/shard_map/all_to_all | solution.py:17
  116.6 0.9 broadcast_in_dim.58
  117.5 3.0 %all-to-all-start.4 = ((bf16[32,16,512]{2,1,0:T(8,128)(2,1)}), bf16[32,16,512]{2,1,0:T(8,128)(2,1)S(1)}, u32[]{:S(2)}, u32[]{:S(2)}) async-start(bf16[32,16,512]{2,1,0:T(8,128)(2,1)} %broadcast_in_dim.58), calls=%async_computation.4 | async-start | bytes 1048576 | tf_op jit(solution)/shard_map/all_to_all | solution.py:41
  120.4 8.3 %fusion.6 = bf16[4096,512]{0,1:T(8,128)(2,1)} fusion(f32[4096,512]{0,1:T(8,128)} %get-tuple-element.27, bf16[4096,512]{0,1:T(8,128)(2,1)} %copy.49, f32[4096]{0:T(1024)S(1)} %get-tuple-element.26, f32[4096]{0:T(1024)S(1)} %add_rsqrt_fusion), kind=kLoop, calls=%fused_computation.8 | loop fusion | flops 12582912 | bytes 16809984 | tf_op jit(solution)/shard_map/convert_element_type | solution.py:83
  128.7 6.4 %copy.51 = bf16[4096,512]{1,0:T(8,128)(2,1)} copy(bf16[4096,512]{0,1:T(8,128)(2,1)} %fusion.6) | data formatting | bytes 8388608
  136.1 1.3 convolution_bitcast_fusion
  (50 shorter events, 17.2 us)
Async XLA Ops:
  0.6 14.9 %copy-start.3 = (bf16[16,12544]{1,0:T(8,128)(2,1)S(1)}, bf16[16,12544]{1,0:T(8,128)(2,1)}, u32[]{:S(2)}) copy-start(bf16[16,12544]{1,0:T(8,128)(2,1)} %param.4) | copy-start | bytes 1204228
  7.3 31.3 %copy-start.4 = (s32[512]{0:T(512)S(1)}, s32[512]{0:T(512)}, u32[]{:S(2)}) copy-start(s32[512]{0:T(512)} %param.7) | copy-start | bytes 6148
  8.2 34.2 %all-to-all-start = ((bf16[32,16,512]{2,1,0:T(8,128)(2,1)}), bf16[32,16,512]{2,1,0:T(8,128)(2,1)S(1)}, u32[]{:S(2)}, u32[]{:S(2)}) async-start(bf16[32,16,512]{2,1,0:T(8,128)(2,1)} %broadcast_in_dim.31), calls=%async_computation | async-start | bytes 1048576 | tf_op jit(solution)/shard_map/all_to_all | solution.py:41
  47.8 3.2 %copy-start.1 = (f32[512,4096]{1,0:T(8,128)}, f32[512,4096]{1,0:T(8,128)S(1)}, u32[]{:S(2)}) copy-start(f32[512,4096]{1,0:T(8,128)S(1)} %get-tuple-element.25) | copy-start | bytes 25165828
  55.8 14.0 %all-to-all-start.1 = ((f32[32,2,512]{2,1,0:T(2,128)}), f32[32,2,512]{2,1,0:T(2,128)S(1)}, u32[]{:S(2)}, u32[]{:S(2)}) async-start(f32[32,2,512]{2,1,0:T(2,128)} %broadcast_in_dim.34), calls=%async_computation.1 | async-start | bytes 262144 | tf_op jit(solution)/shard_map/all_to_all | solution.py:41
  69.9 6.8 %copy-start = (bf16[4096,512]{0,1:T(8,128)(2,1)S(1)}, bf16[4096,512]{0,1:T(8,128)(2,1)}, u32[]{:S(2)}) copy-start(bf16[4096,512]{0,1:T(8,128)(2,1)} %copy.49) | copy-start | bytes 12582916
  76.7 3.2 %copy-start.2 = (bf16[512,4096]{1,0:T(8,128)(2,1)}, bf16[512,4096]{1,0:T(8,128)(2,1)S(1)}, u32[]{:S(2)}) copy-start(bf16[512,4096]{1,0:T(8,128)(2,1)S(1)} %multiply_convert_fusion) | copy-start | bytes 12582916
  79.9 18.2 %all-to-all-start.3 = ((bf16[32,16,512]{2,1,0:T(8,128)(2,1)}), bf16[32,16,512]{2,1,0:T(8,128)(2,1)S(1)}, u32[]{:S(2)}, u32[]{:S(2)}) async-start(bf16[32,16,512]{2,1,0:T(8,128)(2,1)} %bitcast.37), calls=%async_computation.3 | async-start | bytes 1048576 | tf_op jit(solution)/shard_map/all_to_all | solution.py:41
  98.1 18.5 %all-to-all-start.2 = ((bf16[32,16,392]{2,1,0:T(8,128)(2,1)}), bf16[32,16,392]{2,1,0:T(8,128)(2,1)S(1)}, u32[]{:S(2)}, u32[]{:S(2)}) async-start(bf16[32,16,392]{2,1,0:T(8,128)(2,1)} %constant_dynamic-update-slice_fusion), calls=%async_computation.2 | async-start | bytes 1048576 | tf_op jit(solution)/shard_map/all_to_all | solution.py:17
  117.5 18.6 %all-to-all-start.4 = ((bf16[32,16,512]{2,1,0:T(8,128)(2,1)}), bf16[32,16,512]{2,1,0:T(8,128)(2,1)S(1)}, u32[]{:S(2)}, u32[]{:S(2)}) async-start(bf16[32,16,512]{2,1,0:T(8,128)(2,1)} %broadcast_in_dim.58), calls=%async_computation.4 | async-start | bytes 1048576 | tf_op jit(solution)/shard_map/all_to_all | solution.py:41
